TPU v7x, 256 devices: a 8x8x2 block of a 8x8x16 slice. The times are simulated.
256 devices in a mesh: grp: 2 (over z), gx: 64 (over x, y), gz: 2 (over core).
Axes of the slice: x: 8, y: 8, z: 2, core: 2. Of those that a mesh axis runs over, the one named last changes fastest.
The devices are a block of a 8x8x16 slice.
Arguments:
- electric: float32 [4096, 8192], P(('grp', 'gx'), 'gz'), parts along dimension 0, may hold values from -6 to 6
- magnetic_x: float32 [4096, 8192], P(('grp', 'gx'), 'gz'), parts along dimension 0, may hold values from -6 to 6
- magnetic_z: float32 [4096, 8192], P(('grp', 'gx'), 'gz'), parts along dimension 0, may hold values from -6 to 6
- index_map: int32 [4, 64, 8192], P(None, None, 'gz'), may hold values from 0 to 3
- period_seq: int32 [66], P('grp'), parts along dimension 0, may hold values from 0 to 3
- eps_table: float32 [4], replicated, may hold values from 1 to 12.25
- shifts: int32 [8], P('grp'), parts along dimension 0, may hold values from 0 to 4, as said below
Outputs:
- electric_out: float32 [4096, 8192], P(('grp', 'gx'), 'gz'), parts along dimension 0
- magnetic_x_out: float32 [4096, 8192], P(('grp', 'gx'), 'gz'), parts along dimension 0
- magnetic_z_out: float32 [4096, 8192], P(('grp', 'gx'), 'gz'), parts along dimension 0
There are 2 independent parts, one for each index of `grp`. A program takes and returns all parts, laid end to end along the dimension named above; an argument that names none is the same for every part. Nothing has to cross between parts.
Inputs may be any that keep to these rules, and one draw needn't show every extreme that they name: `shifts`: every entry is at most 4, and some entry equals 4.
All inputs are finite; a program needn't handle non-finite values.
Results may differ from a plain program's by a relative error of at most 0.00016.
Values sent between devices are 32-bit elements; how exact they have to be, the bound alone decides.
A program may use at most 64 MiB of HBM per device.

v0:
```python
import jax
import jax.numpy as jnp
from jax import lax
from jax.sharding import PartitionSpec as P

ITERS = 4
SMAX = 4


courant = 0.6


def with_halo(block, sides, width):
    for axis, dim in sides:
        count = lax.axis_size(axis)
        forward = [(i, i + 1) for i in range(count - 1)]
        backward = [(target, source) for source, target in forward]
        low = lax.ppermute(
            lax.slice_in_dim(block, block.shape[dim] - width, None, axis=dim), axis, forward
        )
        high = lax.ppermute(lax.slice_in_dim(block, 0, width, axis=dim), axis, backward)
        block = jnp.concatenate([low, block, high], axis=dim)
    return block


def passed_along(block, axis, distance):
    devices = range(lax.axis_size(axis))
    route = [(i - distance, i) for i in devices if i - distance in devices]
    return lax.ppermute(block, axis, route)


def material(columns, profile, period_seq, inverse):
    span = profile.shape[1]
    period = columns // span
    phase = columns % span
    picked = period[:, None] == jnp.arange(period_seq.shape[0], dtype=jnp.int32)[None, :]
    design = jnp.sum(jnp.where(picked, period_seq[None, :], 0), axis=1)
    rows_all = profile.shape[0] * span
    row_id = design * span + phase
    onehot = (row_id[:, None] == jnp.arange(rows_all, dtype=jnp.int32)[None, :]).astype(jnp.float32)
    table = profile.reshape(rows_all, profile.shape[2]).astype(jnp.float32)
    levels = jnp.dot(onehot, table, precision=lax.Precision.HIGHEST)
    result = jnp.zeros_like(levels)
    for level in range(inverse.shape[0]):
        result = result + jnp.where(levels == level, inverse[level], 0.0)
    return result


def advance(
    extended,
    profile,
    period_seq,
    inverse,
    shifts,
    first,
    count,
    x_start,
    z_start,
    total_x,
    total_z,
    offset,
):
    width = extended.shape[1]
    depth = extended.shape[2]
    tail = jnp.zeros((3, SMAX, depth), extended.dtype)
    columns = x_start + jnp.arange(width, dtype=jnp.int32)
    layers = z_start + jnp.arange(depth, dtype=jnp.int32)
    inside_x = (columns >= 0) & (columns < total_x)
    inside_z = (layers >= 0) & (layers < total_z)
    inside = (inside_x[:, None] & inside_z[None, :]).astype(jnp.float32)
    zero_col = jnp.zeros((width, 1), jnp.float32)
    zero_row = jnp.zeros((1, depth), jnp.float32)
    for step in range(first, first + count):
        moved = shifts[step]
        offset = offset + moved
        extended = lax.dynamic_slice_in_dim(
            jnp.concatenate([extended, tail], axis=1), moved, width, 1
        )
        coeff = material(columns + offset, profile, period_seq, inverse)
        field_e, field_hx, field_hz = (extended[0], extended[1], extended[2])
        upper = jnp.concatenate([field_e[:, 1:], zero_col], axis=1)
        field_hx = (field_hx + courant * (upper - field_e)) * inside
        ahead = jnp.concatenate([field_e[1:], zero_row], axis=0)
        field_hz = (field_hz - courant * (ahead - field_e)) * inside
        lower = jnp.concatenate([zero_col, field_hx[:, :-1]], axis=1)
        behind = jnp.concatenate([zero_row, field_hz[:-1]], axis=0)
        field_e = (field_e + courant * coeff * (field_hx - lower - (field_hz - behind))) * inside
        extended = jnp.stack([field_e, field_hx, field_hz])
    return (extended, offset)


def body(electric, magnetic_x, magnetic_z, index_map, period_seq, eps_table, shifts):
    cells_x, cells_z = electric.shape
    total_x = cells_x * lax.axis_size("gx")
    total_z = cells_z * lax.axis_size("gz")
    first_col = lax.axis_index("gx") * cells_x
    first_layer = lax.axis_index("gz") * cells_z
    inverse = 1.0 / eps_table
    fields = jnp.stack([electric, magnetic_x, magnetic_z])
    offset = jnp.int32(0)
    reach = ITERS * (SMAX + 1)
    profile = with_halo(index_map, (("gz", 2),), ITERS)
    lead = passed_along(fields[:, :reach], "gx", -1)
    trail = passed_along(fields[:, cells_x - ITERS :], "gx", 1)
    extended = jnp.concatenate([trail, fields, lead], axis=1)
    extended = with_halo(extended, (("gz", 2),), ITERS)
    extended, offset = advance(
        extended,
        profile,
        period_seq,
        inverse,
        shifts,
        0,
        ITERS,
        first_col - ITERS,
        first_layer - ITERS,
        total_x,
        total_z,
        offset,
    )
    fields = extended[:, ITERS : ITERS + cells_x, ITERS : ITERS + cells_z]
    return (fields[0], fields[1], fields[2])


def solution(mesh):
    placed = (
        P(("grp", "gx"), "gz"),
        P(("grp", "gx"), "gz"),
        P(("grp", "gx"), "gz"),
        P(None, None, "gz"),
        P("grp"),
        P(),
        P("grp"),
    )
    return jax.shard_map(
        body,
        mesh=mesh,
        in_specs=placed,
        out_specs=(P(("grp", "gx"), "gz"), P(("grp", "gx"), "gz"), P(("grp", "gx"), "gz")),
        check_vma=False,
    )
```

profile of v0, /device:TPU:513, one launch (start us, length us, event | category | flops | bytes accessed | tf_op | source)
XLA Modules:
  0.0 118.9 jit_solution(6135458489412132166)
XLA Ops:
  0.7 1.2 pad_maximum_fusion.3
  1.9 5.3 %collective-permute-start = (f32[3,4,4096]{2,1,0:T(4,128)S(1)}, f32[3,4,4096]{2,1,0:T(4,128)S(1)}, u32[]{:S(2)}, u32[]{:S(2)}) collective-permute-start(f32[3,4,4096]{2,1,0:T(4,128)S(1)} %pad_maximum_fusion.3), channel_id=1, source_target_pairs={{0,2},{2,4},{4,6},{6,8},{8,10},{10,12},{12,14},{14,16},{16,18},{18... | collective-permute-start | bytes 589832 | tf_op jit(solution)/shard_map/ppermute | solution.py:29
  7.2 1.7 %fusion.51 = (s32[4,64,4]{2,1,0:T(8,128)}, s32[4,64,4]{2,1,0:T(8,128)}) fusion(s32[4,64,4096]{2,1,0:T(8,128)} %param.10), kind=kLoop, calls=%fused_computation.133 | loop fusion | bytes 16384 | tf_op jit(solution)/shard_map/slice | solution.py:21
  8.9 18.4 %collective-permute-start.5 = (s32[4,64,4]{2,1,0:T(8,128)}, s32[4,64,4]{2,1,0:T(8,128)S(1)}, u32[]{:S(2)}, u32[]{:S(2)}) collective-permute-start(s32[4,64,4]{2,1,0:T(8,128)} %get-tuple-element.9), channel_id=1, source_target_pairs={{1,0},{3,2},{5,4},{7,6},{9,8},{11,10},{13,12},{15,14},{17,16},{19,... | collective-permute-start | bytes 12296 | tf_op jit(solution)/shard_map/ppermute | solution.py:21
  27.3 1.3 %collective-permute-start.4 = (s32[4,64,4]{2,1,0:T(8,128)}, s32[4,64,4]{2,1,0:T(8,128)S(1)}, u32[]{:S(2)}, u32[]{:S(2)}) collective-permute-start(s32[4,64,4]{2,1,0:T(8,128)} %get-tuple-element.10), channel_id=1, source_target_pairs={{0,1},{2,3},{4,5},{6,7},{8,9},{10,11},{12,13},{14,15},{16,17},{18,... | collective-permute-start | bytes 12296 | tf_op jit(solution)/shard_map/ppermute | solution.py:18
  28.6 2.3 %pad_maximum_fusion.1 = f32[3,20,4096]{2,1,0:T(8,128)} fusion(f32[1,32,4096]{2,1,0:T(8,128)} %bitcast.152, f32[1,32,4096]{2,1,0:T(8,128)} %bitcast.155, f32[1,32,4096]{2,1,0:T(8,128)} %bitcast.158), kind=kLoop, calls=%fused_computation.44 | loop fusion | flops 491520 | bytes 2555904 | tf_op jit(solution)/shard_map/stack | solution.py:99
  30.9 1.3 %collective-permute-start.1 = (f32[3,20,4096]{2,1,0:T(8,128)}, f32[3,20,4096]{2,1,0:T(8,128)S(1)}, u32[]{:S(2)}, u32[]{:S(2)}) collective-permute-start(f32[3,20,4096]{2,1,0:T(8,128)} %pad_maximum_fusion.1), channel_id=1, source_target_pairs={{2,0},{4,2},{6,4},{8,6},{10,8},{12,10},{14,12},{16,14},{18,16},{20... | collective-permute-start | bytes 2949128 | tf_op jit(solution)/shard_map/ppermute | solution.py:29
  32.3 0.7 fusion.53
  33.0 0.6 fusion.54
  35.5 0.7 and_select_fusion.17
  36.9 0.7 fusion.42
  37.7 21.8 %collective-permute-done.1 = f32[3,20,4096]{2,1,0:T(8,128)S(1)} collective-permute-done((f32[3,20,4096]{2,1,0:T(8,128)}, f32[3,20,4096]{2,1,0:T(8,128)S(1)}, u32[]{:S(2)}, u32[]{:S(2)}) %collective-permute-start.1) | collective-permute-done | bytes 983072 | tf_op jit(solution)/shard_map/ppermute | solution.py:29
  59.9 1.6 %copy-done = f32[3,56,4096]{2,1,0:T(8,128)} copy-done((f32[3,56,4096]{2,1,0:T(8,128)}, f32[3,56,4096]{2,1,0:T(8,128)S(1)}, u32[]{:S(2)}) %copy-start) | copy-done | bytes 2752536
  61.6 3.9 %collective-permute-start.3 = (f32[3,56,4]{2,1,0:T(8,128)S(1)}, f32[3,56,4]{2,1,0:T(8,128)S(1)}, u32[]{:S(2)}, u32[]{:S(2)}) collective-permute-start(f32[3,56,4]{2,1,0:T(8,128)S(1)} %get-tuple-element.17), channel_id=1, source_target_pairs={{1,0},{3,2},{5,4},{7,6},{9,8},{11,10},{13,12},{15,14},{17,16},{19,... | collective-permute-start | bytes 8072 | tf_op jit(solution)/shard_map/ppermute | solution.py:21
  65.5 1.3 %collective-permute-start.2 = (f32[3,56,4]{2,1,0:T(8,128)S(1)}, f32[3,56,4]{2,1,0:T(8,128)S(1)}, u32[]{:S(2)}, u32[]{:S(2)}) collective-permute-start(f32[3,56,4]{2,1,0:T(8,128)S(1)} %get-tuple-element.18), channel_id=1, source_target_pairs={{0,1},{2,3},{4,5},{6,7},{8,9},{10,11},{12,13},{14,15},{16,17},{18,... | collective-permute-start | bytes 8072 | tf_op jit(solution)/shard_map/ppermute | solution.py:18
  74.4 6.4 %concatenate.72 = s32[4,64,4104]{2,1,0:T(8,128)} concatenate(s32[4,64,4]{2,1,0:T(8,128)S(1)} %collective-permute-done.4, s32[4,64,4096]{2,1,0:T(8,128)} %param.10, s32[4,64,4]{2,1,0:T(8,128)S(1)} %collective-permute-done.5), dimensions={2} | concatenate | bytes 8404992 | tf_op jit(solution)/shard_map/concatenate | solution.py:22
  80.8 4.5 %convert_element_type.5 = f32[4,64,4104]{2,1,0:T(8,128)} convert(s32[4,64,4104]{2,1,0:T(8,128)} %concatenate.72) | non-fusion elementwise | flops 1050624 | bytes 8404992 | tf_op jit(solution)/shard_map/convert_element_type | solution.py:41
  85.4 3.5 %concatenate.70 = f32[3,56,4104]{2,1,0:T(8,128)S(1)} concatenate(f32[3,56,4]{2,1,0:T(8,128)S(1)} %collective-permute-done.2, f32[3,56,4096]{2,1,0:T(8,128)} %copy-done, f32[3,56,4]{2,1,0:T(8,128)S(1)} %collective-permute-done.3), dimensions={2} | concatenate | bytes 5515776 | tf_op jit(solution)/shard_map/concatenate | solution.py:22
  89.9 1.2 %slice-done = s8[4194304]{0:T(1024)(128)(4,1)S(1)} async-done(((s8[4325376]{0:T(1024)(128)(4,1)}), s8[4194304]{0:T(1024)(128)(4,1)S(1)}, s32[]{:S(2)}) %slice-start) | async-done | bytes 4194328
  91.2 5.0 %fusion.21 = f32[1,56,4104]{2,1,0:T(8,128)S(1)} fusion(f32[56,4104]{1,0:T(8,128)S(1)} %get-tuple-element.8, f32[56,4104]{1,0:T(8,128)S(1)} %get-tuple-element.7, f32[55,4104]{1,0:T(8,128)S(1)} %bitcast.135, f32[56,4104]{1,0:T(8,128)S(1)} %and_select_fusion.11, f32[56,4103]{1,0:T(8,128)S(1)} %bitcast.137, f32[]{:T(128)} %bitcast.9, f32[]{:T(128)} %bitcast.8, ...), kind=kOutput, calls=%fused_computation.52 | convolution fusion | flops 710400320 | bytes 9706032 | tf_op jit(solution)/shard_map/dot_general | solution.py:42
  96.3 0.5 fusion.2
  97.2 0.4 and_select_fusion.8
  97.7 5.1 %fusion.22 = f32[1,56,4104]{2,1,0:T(8,128)S(1)} fusion(f32[56,4104]{1,0:T(8,128)S(1)} %get-tuple-element.16, f32[55,4104]{1,0:T(8,128)S(1)} %bitcast.141, f32[56,4104]{1,0:T(8,128)S(1)} %get-tuple-element.15, f32[56,4103]{1,0:T(8,128)S(1)} %bitcast.139, f32[]{:T(128)} %bitcast.9, f32[]{:T(128)} %bitcast.8, f32[]{:T(128)} %bitcast.7, f32[]{:T(128)} %bitcast.6, ...), kind=kOutput, calls=%fused_computation.53 | convolution fusion | flops 710400320 | bytes 9706032 | tf_op jit(solution)/shard_map/dot_general | solution.py:42
  102.8 0.5 fusion.7
  103.8 0.4 and_select_fusion.5
  104.2 5.1 %fusion.23 = f32[1,56,4104]{2,1,0:T(8,128)S(1)} fusion(f32[56,4104]{1,0:T(8,128)S(1)} %get-tuple-element.14, f32[55,4104]{1,0:T(8,128)S(1)} %bitcast.145, f32[56,4104]{1,0:T(8,128)S(1)} %get-tuple-element.13, f32[56,4103]{1,0:T(8,128)S(1)} %bitcast.143, f32[]{:T(128)} %bitcast.9, f32[]{:T(128)} %bitcast.8, f32[]{:T(128)} %bitcast.7, f32[]{:T(128)} %bitcast.6, ...), kind=kOutput, calls=%fused_computation.54 | convolution fusion | flops 710400320 | bytes 9706032 | tf_op jit(solution)/shard_map/dot_general | solution.py:42
  109.3 0.5 fusion.12
  110.3 0.6 and_select_fusion.2
  110.9 5.0 %fusion.24 = f32[1,56,4104]{2,1,0:T(8,128)S(1)} fusion(f32[56,4104]{1,0:T(8,128)S(1)} %get-tuple-element.12, f32[55,4104]{1,0:T(8,128)S(1)} %bitcast.149, f32[56,4104]{1,0:T(8,128)S(1)} %get-tuple-element.11, f32[56,4103]{1,0:T(8,128)S(1)} %bitcast.147, f32[]{:T(128)} %bitcast.9, f32[]{:T(128)} %bitcast.8, f32[]{:T(128)} %bitcast.7, f32[]{:T(128)} %bitcast.6, ...), kind=kOutput, calls=%fused_computation.55 | convolution fusion | flops 710400320 | bytes 9706032 | tf_op jit(solution)/shard_map/dot_general | solution.py:42
  115.9 1.0 slice_bitcast_fusion.14
  116.9 1.0 slice_bitcast_fusion.12
  117.9 1.0 slice_bitcast_fusion.13
  (45 shorter events, 3.1 us)
Async XLA Ops:
  0.6 58.8 %copy-start.1 = (f32[32,4096]{1,0:T(8,128)S(1)}, f32[32,4096]{1,0:T(8,128)}, u32[]{:S(2)}) copy-start(f32[32,4096]{1,0:T(8,128)} %param.9) | copy-start | bytes 1572868
  0.6 58.8 %copy-start.2 = (f32[32,4096]{1,0:T(8,128)S(1)}, f32[32,4096]{1,0:T(8,128)}, u32[]{:S(2)}) copy-start(f32[32,4096]{1,0:T(8,128)} %param.8) | copy-start | bytes 1572868
  0.7 58.8 %copy-start.3 = (f32[32,4096]{1,0:T(8,128)S(1)}, f32[32,4096]{1,0:T(8,128)}, u32[]{:S(2)}) copy-start(f32[32,4096]{1,0:T(8,128)} %param.7) | copy-start | bytes 1572868
  0.7 31.6 %copy-start.6 = (f32[4]{0:T(128)S(1)}, f32[4]{0:T(128)}, u32[]{:S(2)}) copy-start(f32[4]{0:T(128)} %param.12) | copy-start | bytes 52
  0.7 32.3 %copy-start.4 = (s32[4]{0:T(128)S(1)}, s32[4]{0:T(128)}, u32[]{:S(2)}) copy-start(s32[4]{0:T(128)} %param.13) | copy-start | bytes 52
  0.7 36.1 %copy-start.5 = (s32[33]{0:T(128)S(1)}, s32[33]{0:T(128)}, u32[]{:S(2)}) copy-start(s32[33]{0:T(128)} %param.11) | copy-start | bytes 400
  1.9 35.8 %collective-permute-start = (f32[3,4,4096]{2,1,0:T(4,128)S(1)}, f32[3,4,4096]{2,1,0:T(4,128)S(1)}, u32[]{:S(2)}, u32[]{:S(2)}) collective-permute-start(f32[3,4,4096]{2,1,0:T(4,128)S(1)} %pad_maximum_fusion.3), channel_id=1, source_target_pairs={{0,2},{2,4},{4,6},{6,8},{8,10},{10,12},{12,14},{14,16},{16,18},{18... | collective-permute-start | bytes 589832 | tf_op jit(solution)/shard_map/ppermute | solution.py:29
  8.9 65.5 %collective-permute-start.5 = (s32[4,64,4]{2,1,0:T(8,128)}, s32[4,64,4]{2,1,0:T(8,128)S(1)}, u32[]{:S(2)}, u32[]{:S(2)}) collective-permute-start(s32[4,64,4]{2,1,0:T(8,128)} %get-tuple-element.9), channel_id=1, source_target_pairs={{1,0},{3,2},{5,4},{7,6},{9,8},{11,10},{13,12},{15,14},{17,16},{19,... | collective-permute-start | bytes 12296 | tf_op jit(solution)/shard_map/ppermute | solution.py:21
  27.3 47.1 %collective-permute-start.4 = (s32[4,64,4]{2,1,0:T(8,128)}, s32[4,64,4]{2,1,0:T(8,128)S(1)}, u32[]{:S(2)}, u32[]{:S(2)}) collective-permute-start(s32[4,64,4]{2,1,0:T(8,128)} %get-tuple-element.10), channel_id=1, source_target_pairs={{0,1},{2,3},{4,5},{6,7},{8,9},{10,11},{12,13},{14,15},{16,17},{18,... | collective-permute-start | bytes 12296 | tf_op jit(solution)/shard_map/ppermute | solution.py:18
  30.9 28.5 %collective-permute-start.1 = (f32[3,20,4096]{2,1,0:T(8,128)}, f32[3,20,4096]{2,1,0:T(8,128)S(1)}, u32[]{:S(2)}, u32[]{:S(2)}) collective-permute-start(f32[3,20,4096]{2,1,0:T(8,128)} %pad_maximum_fusion.1), channel_id=1, source_target_pairs={{2,0},{4,2},{6,4},{8,6},{10,8},{12,10},{14,12},{16,14},{18,16},{20... | collective-permute-start | bytes 2949128 | tf_op jit(solution)/shard_map/ppermute | solution.py:29
  59.9 1.6 %copy-start = (f32[3,56,4096]{2,1,0:T(8,128)}, f32[3,56,4096]{2,1,0:T(8,128)S(1)}, u32[]{:S(2)}) copy-start(f32[3,56,4096]{2,1,0:T(8,128)S(1)} %pad_maximum_fusion) | copy-start | bytes 8257540
  61.6 23.8 %collective-permute-start.3 = (f32[3,56,4]{2,1,0:T(8,128)S(1)}, f32[3,56,4]{2,1,0:T(8,128)S(1)}, u32[]{:S(2)}, u32[]{:S(2)}) collective-permute-start(f32[3,56,4]{2,1,0:T(8,128)S(1)} %get-tuple-element.17), channel_id=1, source_target_pairs={{1,0},{3,2},{5,4},{7,6},{9,8},{11,10},{13,12},{15,14},{17,16},{19,... | collective-permute-start | bytes 8072 | tf_op jit(solution)/shard_map/ppermute | solution.py:21
  65.5 19.8 %collective-permute-start.2 = (f32[3,56,4]{2,1,0:T(8,128)S(1)}, f32[3,56,4]{2,1,0:T(8,128)S(1)}, u32[]{:S(2)}, u32[]{:S(2)}) collective-permute-start(f32[3,56,4]{2,1,0:T(8,128)S(1)} %get-tuple-element.18), channel_id=1, source_target_pairs={{0,1},{2,3},{4,5},{6,7},{8,9},{10,11},{12,13},{14,15},{16,17},{18,... | collective-permute-start | bytes 8072 | tf_op jit(solution)/shard_map/ppermute | solution.py:18
  89.0 2.2 %slice-start = ((s8[4325376]{0:T(1024)(128)(4,1)}), s8[4194304]{0:T(1024)(128)(4,1)S(1)}, s32[]{:S(2)}) async-start(s8[4325376]{0:T(1024)(128)(4,1)} %bitcast.129), calls=%async_computation | async-start | bytes 8388608
  89.3 1.9 %slice-start.1 = ((s8[4325376]{0:T(1024)(128)(4,1)}), s8[131072]{0:T(1024)(128)(4,1)S(1)}, s32[]{:S(2)}) async-start(s8[4325376]{0:T(1024)(128)(4,1)} %bitcast.129), calls=%async_computation.1 | async-start | bytes 262144
where the time goes:
time: 120 us; the launch traced here: 119 us
  starting transfers between devices  31.5 us (26%)
  waiting for transfers between devices  21.8 us (18%)
  local copies, waits for them, and re-layouts  20.6 us (17%)
  matrix products  20.2 us (17%)
  other arithmetic  13.7 us (11%)
  between operations  11.1 us (9%)
    ppermute x2, starting transfers between devices, with_halo(): lax.ppermute(lax.slice_in_dim(block, 0, width, axis=dim), axis, backward)  22.3 us
    ppermute x2, waiting for transfers between devices, passed_along(): return lax.ppermute(block, axis, route)  21.8 us
    dot_general x4, matrix products, material(): levels = jnp.dot(onehot, table, precision=lax.Precision.HIGHEST)  20.2 us
    concatenate x2, local copies, waits for them, and re-layouts, with_halo(): block = jnp.concatenate([low, block, high], axis=dim)  9.92 us
    ppermute x2, starting transfers between devices, passed_along(): return lax.ppermute(block, axis, route)  6.56 us
    convert_element_type x1, other arithmetic, material(): table = profile.reshape(rows_all, profile.shape[2]).astype(jnp.float32)  4.51 us
    squeeze x3, local copies, waits for them, and re-layouts, body(): return (fields[0], fields[1], fields[2])  2.99 us
    unnamed x18, local copies, waits for them, and re-layouts  2.88 us
  transfers between devices with their start and end apart: 6, of which 1 were waited for; matrix products, arithmetic and copies ran while one was open for 15% of the time, Pallas kernels for 0%

commit v1 on v0

v1 whole, which is shorter than its diff:
```python
import functools

import jax
import jax.numpy as jnp
from jax import lax
from jax.experimental import pallas as pl
from jax.experimental.pallas import tpu as pltpu
from jax.sharding import PartitionSpec as P

ITERS = 4
SMAX = 4
COURANT = 0.6
MESH = pl.DeviceIdType.MESH

LANE = 128
PAD = 5
CHUNK = 4
REACH = ITERS * SMAX
EARLY = 2


def kernel(
    rows,
    own,
    span,
    shifts_ref,
    seq_ref,
    eps_ref,
    e_in,
    hx_in,
    hz_in,
    map_in,
    e_out,
    hx_out,
    hz_out,
    e0,
    hx0,
    hz0,
    e1,
    hx1,
    hz1,
    e2,
    hx2,
    hz2,
    e3,
    hx3,
    hz3,
    e4,
    hx4,
    hz4,
    coeff,
    design_rows,
    edge_rows,
    bound_out,
    bound_in,
    local_sem,
    edge_send,
    edge_recv,
    send_sem,
    recv_sem,
    bound_send_sem,
    bound_recv_sem,
    relay_send,
    relay_recv,
):
    me = lax.axis_index("gx")
    core = lax.axis_index("gz")
    count = lax.axis_size("gx")
    left = lax.rem(me + count - 1, count)
    right = lax.rem(me + 1, count)
    total = rows + REACH
    bands = total // 8
    own_bands = rows // 8
    chunks = own // CHUNK
    cells = own * LANE
    is_last = me == count - 1

    to_left = {"gx": left}
    to_right = {"gx": right}
    to_partner = {"gz": 1 - core}

    ins = (e_in, hx_in, hz_in)
    state = ((e0, hx0, hz0), (e1, hx1, hz1), (e2, hx2, hz2), (e3, hx3, hz3), (e4, hx4, hz4))
    start = state[0]
    mine = pl.ds(PAD * LANE, cells)

    def at(tile):
        return pl.ds(pl.multiple_of(tile * LANE, LANE), LANE)

    phase = lax.rem(me * rows, span)
    high = lax.rem(me * rows + rows, span)
    loads = [
        pltpu.make_async_copy(ins[f], start[f].at[pl.ds(0, rows), mine], local_sem.at[f])
        for f in range(3)
    ]
    loads.append(
        pltpu.make_async_copy(
            map_in.at[:, pl.ds(pl.multiple_of(phase, 8), rows), :],
            design_rows.at[:, pl.ds(0, rows), :],
            local_sem.at[3],
        )
    )
    loads.append(
        pltpu.make_async_copy(
            map_in.at[:, pl.ds(pl.multiple_of(high, 8), REACH), :],
            design_rows.at[:, pl.ds(rows, REACH), :],
            local_sem.at[4],
        )
    )
    for load in loads:
        load.start()

    barrier = pltpu.get_barrier_semaphore()
    pl.semaphore_signal(barrier, inc=1, device_id=to_right, device_id_type=MESH)
    pl.semaphore_signal(barrier, inc=1, device_id=to_partner, device_id_type=MESH)
    pl.semaphore_wait(barrier, 2)

    edge = (1 - core) * (own - 1)
    halo = jnp.where(core == 1, PAD + own, PAD - 1)
    here = jnp.where(core == 0, PAD + own, PAD - 1)
    outside = jnp.where(core == 1, PAD + own, PAD - 1)

    def remote(src, dst, send, recv, target):
        return pltpu.make_async_remote_copy(
            src_ref=src, dst_ref=dst, send_sem=send, recv_sem=recv, device_id=target, device_id_type=MESH
        )

    def bulk(f, first, width, slot):
        source = pl.ds(pl.multiple_of(first * LANE, LANE), width * LANE)
        target = pl.ds(pl.multiple_of((first + PAD) * LANE, LANE), width * LANE)
        return remote(
            ins[f].at[pl.ds(0, REACH), source],
            start[f].at[pl.ds(rows, REACH), target],
            send_sem.at[f, slot],
            recv_sem.at[f, slot],
            to_left,
        )

    def chunk_copy(f, j):
        if isinstance(j, int) and j == chunks - 1:
            return bulk(f, core + j * CHUNK, CHUNK - 1, j)
        return bulk(f, core + j * CHUNK, CHUNK, j)

    edge_copies = [bulk(f, edge, 1, chunks) for f in range(3)]
    partner_copies = [
        remote(
            ins[f].at[:, at(edge)],
            start[f].at[pl.ds(0, rows), at(halo)],
            edge_send.at[f],
            edge_recv.at[f],
            to_partner,
        )
        for f in range(3)
    ]
    partner_copies.append(
        remote(
            map_in.at[:, pl.ds(pl.multiple_of(phase, 8), rows), at(edge)],
            edge_rows.at[:, pl.ds(0, rows), :],
            edge_send.at[3],
            edge_recv.at[3],
            to_partner,
        )
    )
    partner_copies.append(
        remote(
            map_in.at[:, pl.ds(pl.multiple_of(high, 8), REACH), at(edge)],
            edge_rows.at[:, pl.ds(rows, REACH), :],
            edge_send.at[4],
            edge_recv.at[4],
            to_partner,
        )
    )
    for copy in edge_copies:
        copy.start()
    for copy in partner_copies:
        copy.start()
    for j in range(EARLY):
        for f in range(3):
            chunk_copy(f, j).start()

    lane = lax.broadcasted_iota(jnp.int32, (8, LANE), 1)
    sub = lax.broadcasted_iota(jnp.int32, (8, LANE), 0)
    zero = jnp.zeros((8, LANE), jnp.float32)
    last_vec = jnp.full((8, LANE), me, jnp.int32) == count - 1
    offsets = []
    offset = jnp.int32(0)
    for step in range(ITERS):
        offset = offset + shifts_ref[step]
        offsets.append(offset)

    for f in range(3):
        for r in range(bands):
            start[f][pl.ds(8 * r, 8), at(outside)] = zero

    gains = [COURANT * (1.0 / jnp.full((8, LANE), eps_ref[k], jnp.float32)) for k in range(4)]
    period = me * rows // span
    next_period = (me * rows + rows) // span
    designs = [jnp.full((8, LANE), seq_ref[p], jnp.int32) for p in (period, next_period)]

    def gain_of(level):
        return jnp.where(
            level < 2,
            jnp.where(level == 0, gains[0], gains[1]),
            jnp.where(level == 2, gains[2], gains[3]),
        )

    def gain_tile(source, r, tile, target):
        design = designs[0] if r < own_bands else designs[1]
        maps = [source[k, pl.ds(8 * r, 8), at(tile)] for k in range(source.shape[0])]
        level = maps[0]
        for k in range(1, len(maps)):
            level = jnp.where(design == k, maps[k], level)
        coeff[pl.ds(8 * r, 8), at(target)] = gain_of(level)

    def gain_bands(which):
        def body(tile, carry):
            for r in which:
                gain_tile(design_rows, r, tile, tile + PAD)
            return carry

        lax.fori_loop(0, own, body, 0, unroll=2)
        for r in which:
            gain_tile(edge_rows, r, 0, here)

    def load(ref, r, tile):
        return ref[pl.ds(8 * r, 8), at(tile)]

    def advance(j, s, which, main):
        old, new = state[s - 1], state[s]
        base = CHUNK * j + PAD - s
        ahead_tiles = [[load(old[0], r, base + i) for r in which] for i in range(CHUNK + 1)]
        if main and s == 1:
            ahead_tiles = [
                [jnp.where(last_vec, 0.0, v) if r >= own_bands else v for r, v in zip(which, tile)]
                for tile in ahead_tiles
            ]
        hx_low = [load(new[1], r, base - 1) for r in which]
        cut_low = jnp.full((8, LANE), core * 1024 + j, jnp.int32) == 0
        cut_high = jnp.full((8, LANE), (1 - core) * 1024 + chunks - j, jnp.int32) == 0
        for i in range(CHUNK):
            tile = base + i
            e_now, e_right = ahead_tiles[i], ahead_tiles[i + 1]
            hx_new, hz_new = [], []
            bound = None
            if main:
                row = bound_in[pl.ds(s - 1, 1), at(tile)]
                bound = jnp.where(last_vec, 0.0, jnp.broadcast_to(row, (8, LANE)))
            for k, r in enumerate(which):
                e = e_now[k]
                hx = load(old[1], r, tile)
                hz = load(old[2], r, tile)
                if main and s == 1 and r >= own_bands:
                    hx = jnp.where(last_vec, 0.0, hx)
                    hz = jnp.where(last_vec, 0.0, hz)
                upper = pltpu.roll(jnp.where(lane == 0, e_right[k], e), LANE - 1, 1)
                hx = hx + COURANT * (upper - e)
                following = e_now[k + 1] if k + 1 < len(which) else (bound if main else zero)
                beyond = pltpu.roll(jnp.where(sub == 0, following, e), 7, 0)
                hz = hz - COURANT * (beyond - e)
                if i == s - 1:
                    hx = jnp.where(cut_low, 0.0, hx)
                if main and r < REACH // 8:
                    inside = sub + (me * rows + 8 * r) >= offsets[s - 1]
                    hz = jnp.where(inside, hz, 0.0)
                if main and r >= own_bands:
                    inside = sub + (me * rows + 8 * r) < offsets[s - 1] + count * rows
                    hx = jnp.where(inside, hx, 0.0)
                    hz = jnp.where(inside, hz, 0.0)
                hx_new.append(hx)
                hz_new.append(hz)
            for k, r in enumerate(which):
                e, hx, hz = e_now[k], hx_new[k], hz_new[k]
                lower = pltpu.roll(jnp.where(lane == LANE - 1, hx_low[k], hx), 1, 1)
                before = hz_new[k - 1] if k > 0 else zero
                behind = pltpu.roll(jnp.where(sub == 7, before, hz), 1, 0)
                e = e + load(coeff, r, tile) * ((hx - lower) - (hz - behind))
                if i == s:
                    e = jnp.where(cut_high, 0.0, e)
                if main and r >= own_bands:
                    inside = sub + (me * rows + 8 * r) < offsets[s - 1] + count * rows
                    e = jnp.where(inside, e, 0.0)
                new[0][pl.ds(8 * r, 8), at(tile)] = e
                new[1][pl.ds(8 * r, 8), at(tile)] = hx
                new[2][pl.ds(8 * r, 8), at(tile)] = hz
                if not main and r == REACH // 8:
                    bound_out[pl.ds(s, 1), at(tile)] = e[0:1]
                    if s == 1:
                        bound_out[pl.ds(0, 1), at(tile)] = e_now[k][0:1]
            hx_low = hx_new

    strip = [REACH // 8 - 1, REACH // 8]
    for load_copy in loads:
        load_copy.wait()
    for copy in partner_copies:
        copy.wait_recv()
    gain_bands(strip)

    def strip_chunk(j, carry):
        for s in range(1, ITERS):
            advance(j, s, strip, False)
        return carry

    lax.fori_loop(0, chunks + 1, strip_chunk, 0)
    gain_bands([r for r in range(bands) if r not in strip])
    bound_copy = remote(
        bound_out.at[:, mine], bound_in.at[:, mine], bound_send_sem, bound_recv_sem, to_left
    )
    bound_copy.start()
    for j in range(EARLY, chunks):
        for f in range(3):
            chunk_copy(f, j).start()

    relays = [
        remote(
            start[f].at[pl.ds(rows, REACH), at(edge + PAD)],
            start[f].at[pl.ds(rows, REACH), at(halo)],
            relay_send.at[f],
            relay_recv.at[f],
            to_partner,
        )
        for f in range(3)
    ]
    relays.append(
        remote(
            bound_in.at[:, at(edge + PAD)],
            bound_in.at[:, at(halo)],
            relay_send.at[3],
            relay_recv.at[3],
            to_partner,
        )
    )
    for f in range(3):
        edge_copies[f].wait_recv()
        relays[f].start()
    bound_copy.wait_recv()
    relays[3].start()
    for copy in relays:
        copy.wait_recv()

    moved = offsets[-1]
    turn = jnp.bitwise_and(moved, 7)
    back = jnp.bitwise_and(8 - turn, 7)
    moved_vec = jnp.full((8, LANE), moved, jnp.int32)
    turned = sub < jnp.full((8, LANE), turn, jnp.int32)
    everything = list(range(bands))
    outs = (e_out, hx_out, hz_out)

    def finish(j):
        for i in range(CHUNK):
            tile = CHUNK * j + PAD - ITERS + i
            for f in range(3):
                lines = [load(state[ITERS][f], r, tile) for r in range(bands)]
                for k in range(1, REACH // 8 + 1):
                    lines = [
                        jnp.where(moved_vec >= 8 * k, lines[r + 1], lines[r]) if r + 1 < bands else lines[r]
                        for r in range(bands)
                    ]
                for r in range(own_bands):
                    joined = jnp.where(turned, lines[r + 1], lines[r])
                    outs[f][pl.ds(8 * r, 8), at(tile - PAD)] = pltpu.roll(joined, back, 0)

    def main_chunk(j):
        for s in range(1, ITERS + 1):
            advance(j, s, everything, True)

    def first_chunk():
        for f in range(3):
            chunk_copy(f, 0).wait_recv()
        main_chunk(jnp.int32(0))

    def middle(j, carry):
        for f in range(3):
            chunk_copy(f, j).wait_recv()
        main_chunk(j)
        finish(j)
        return carry

    first_chunk()
    lax.fori_loop(1, chunks - 1, middle, 0)
    for f in range(3):
        chunk_copy(f, chunks - 1).wait_recv()

    def closing(j, carry):
        main_chunk(j)
        finish(j)
        return carry

    lax.fori_loop(chunks - 1, chunks + 1, closing, 0)

    for copy in edge_copies + partner_copies + relays + [bound_copy]:
        copy.wait_send()
    for j in range(chunks):
        for f in range(3):
            chunk_copy(f, j).wait_send()


def body(electric, magnetic_x, magnetic_z, index_map, period_seq, eps_table, shifts):
    rows, cells = electric.shape
    own = cells // LANE
    width = (PAD + own + CHUNK) * LANE
    total = rows + REACH
    chunks = own // CHUNK
    types, span, _ = index_map.shape
    field = pltpu.VMEM((total, width), jnp.float32)
    dma = pltpu.SemaphoreType.DMA
    hbm = pl.BlockSpec(memory_space=pl.ANY)
    smem = pl.BlockSpec(memory_space=pltpu.SMEM)
    vmem = pl.BlockSpec(memory_space=pltpu.VMEM)
    out = jax.ShapeDtypeStruct((rows, cells), jnp.float32)
    return pl.pallas_call(
        functools.partial(kernel, rows, own, span),
        out_shape=(out, out, out),
        in_specs=[smem, smem, smem, hbm, hbm, hbm, hbm],
        out_specs=(vmem, vmem, vmem),
        scratch_shapes=[field] * 16
        + [
            pltpu.VMEM((types, total, cells), jnp.int32),
            pltpu.VMEM((types, total, LANE), jnp.int32),
            pltpu.VMEM((ITERS, width), jnp.float32),
            pltpu.VMEM((ITERS, width), jnp.float32),
            dma((5,)),
            dma((5,)),
            dma((5,)),
            dma((3, chunks + 1)),
            dma((3, chunks + 1)),
            dma,
            dma,
            dma((4,)),
            dma((4,)),
        ],
        compiler_params=pltpu.CompilerParams(
            collective_id=0, has_side_effects=True, vmem_limit_bytes=48 * 1024 * 1024
        ),
        name="yee",
    )(shifts, period_seq, eps_table, electric, magnetic_x, magnetic_z, index_map)


def solution(mesh):
    field = P(("grp", "gx"), "gz")
    placed = (field, field, field, P(None, None, "gz"), P("grp"), P(), P("grp"))
    return jax.shard_map(
        body, mesh=mesh, in_specs=placed, out_specs=(field, field, field), check_vma=False
    )
```

time: 120 us -> 53.3 us (0.44)
  Pallas kernels: 0 us -> 44.9 us
  starting transfers between devices: 31.5 us -> 0 us
  waiting for transfers between devices: 21.8 us -> 0 us
  matrix products: 20.2 us -> 0 us
  other arithmetic: 13.7 us -> 0 us
  local copies, waits for them, and re-layouts: 20.6 us -> 7.46 us
  between operations: 11.1 us -> 0.66 us
    pallas_call x0 -> x1, Pallas kernels: none -> 44.9 us  [body(): pl.pallas_call(functools.partial(kernel, rows, own, span), out_shape=(out...]
    ppermute x6 -> x0, starting transfers between devices: 31.5 us -> none  [the longest x2 22.3 us: with_halo(): lax.ppermute(lax.slice_in_dim(block, 0, width, axis=dim), axis, backward)]
    ppermute x6 -> x0, waiting for transfers between devices: 21.8 us -> none  [the longest x2 21.8 us: passed_along(): return lax.ppermute(block, axis, route)]
    dot_general x4 -> x0, matrix products: 20.2 us -> none  [material(): levels = jnp.dot(onehot, table, precision=lax.Precision.HIGHEST)]
    concatenate x2 -> x0, local copies, waits for them, and re-layouts: 9.92 us -> none  [with_halo(): block = jnp.concatenate([low, block, high], axis=dim)]
    slice x12 -> x0, local copies, waits for them, and re-layouts: 4.66 us -> none  [the longest x2 1.81 us: with_halo(): lax.slice_in_dim(block, 0, width, axis=dim)]
    unnamed x18 -> x15, local copies, waits for them, and re-layouts: 2.88 us -> 7.46 us
    convert_element_type x1 -> x0, other arithmetic: 4.51 us -> none  [material(): table = profile.reshape(rows_all, profile.shape[2]).astype(jnp.float32)]
  transfers between devices with their start and end apart: 6 -> 0, of which waited for: 1 -> 0; matrix products, arithmetic and copies ran while one was open for 15% -> 0% of each run, Pallas kernels for 0% -> 0%
where the time goes in v1:
time: 53.3 us; the launch traced here: 53 us
  Pallas kernels  44.9 us (84%)
  local copies, waits for them, and re-layouts  7.46 us (14%)
  between operations  0.66 us (1%)
    pallas_call x1, Pallas kernels, body(): pl.pallas_call(functools.partial(kernel, rows, own, span), out_shape=(out...  44.9 us
    unnamed x15, local copies, waits for them, and re-layouts  7.46 us

profile of v1, /device:TPU:513, one launch (start us, length us, event | category | flops | bytes accessed | tf_op | source)
XLA Modules:
  0.0 53.0 jit_solution(15728143278096907933)
XLA Ops:
  0.6 0.0 copy-start
  0.6 1.0 %copy-done = f32[32,4096]{1,0:T(8,128)S(1)} copy-done((f32[32,4096]{1,0:T(8,128)S(1)}, f32[32,4096]{1,0:T(8,128)}, u32[]{:S(2)}) %copy-start) | copy-done | bytes 524312
  1.7 0.0 copy-start.1
  1.7 1.0 %copy-done.1 = f32[32,4096]{1,0:T(8,128)S(1)} copy-done((f32[32,4096]{1,0:T(8,128)S(1)}, f32[32,4096]{1,0:T(8,128)}, u32[]{:S(2)}) %copy-start.1) | copy-done | bytes 524312
  2.7 0.0 copy-start.2
  2.7 1.0 %copy-done.2 = f32[32,4096]{1,0:T(8,128)S(1)} copy-done((f32[32,4096]{1,0:T(8,128)S(1)}, f32[32,4096]{1,0:T(8,128)}, u32[]{:S(2)}) %copy-start.2) | copy-done | bytes 524312
  3.8 0.0 copy-start.3
  3.8 0.7 %copy-done.3 = s32[4]{0:T(128)S(1)} copy-done((s32[4]{0:T(128)S(1)}, s32[4]{0:T(128)}, u32[]{:S(2)}) %copy-start.3) | copy-done | bytes 40
  4.4 0.0 copy-start.4
  4.4 0.7 %copy-done.4 = s32[33]{0:T(128)S(1)} copy-done((s32[33]{0:T(128)S(1)}, s32[33]{0:T(128)}, u32[]{:S(2)}) %copy-start.4) | copy-done | bytes 156
  5.1 0.0 copy-start.5
  5.1 0.7 %copy-done.5 = f32[4]{0:T(128)S(1)} copy-done((f32[4]{0:T(128)S(1)}, f32[4]{0:T(128)}, u32[]{:S(2)}) %copy-start.5) | copy-done | bytes 40
  5.7 44.9 %yee.1 = (f32[32,4096]{1,0:T(8,128)S(1)}, f32[32,4096]{1,0:T(8,128)S(1)}, f32[32,4096]{1,0:T(8,128)S(1)}) custom-call(s32[4]{0:T(128)S(1)} %copy-done.3, s32[33]{0:T(128)S(1)} %copy-done.4, f32[4]{0:T(128)S(1)} %copy-done.5, f32[32,4096]{1,0:T(8,128)S(1)} %copy-done, f32[32,4096]{1,0:T(8,128)S(1)} %copy-done.1, f32[32,4096]{1,0:T(8,128)S(1)} %copy-done.2, ...), custom_call_target="tpu_custom_call" | custom-call | tf_op jit(solution)/shard_map/yee/pallas_call | solution.py:410
  50.6 0.8 %copy.13 = f32[32,4096]{1,0:T(8,128)} copy(f32[32,4096]{1,0:T(8,128)S(1)} %get-tuple-element.6) | data formatting | bytes 1048576
  51.4 0.8 %copy.14 = f32[32,4096]{1,0:T(8,128)} copy(f32[32,4096]{1,0:T(8,128)S(1)} %get-tuple-element.7) | data formatting | bytes 1048576
  52.2 0.8 %copy.15 = f32[32,4096]{1,0:T(8,128)} copy(f32[32,4096]{1,0:T(8,128)S(1)} %get-tuple-element.8) | data formatting | bytes 1048576
Async XLA Ops:
  0.6 1.0 %copy-start = (f32[32,4096]{1,0:T(8,128)S(1)}, f32[32,4096]{1,0:T(8,128)}, u32[]{:S(2)}) copy-start(f32[32,4096]{1,0:T(8,128)} %e_in.1) | copy-start | bytes 1572868
  1.7 1.0 %copy-start.1 = (f32[32,4096]{1,0:T(8,128)S(1)}, f32[32,4096]{1,0:T(8,128)}, u32[]{:S(2)}) copy-start(f32[32,4096]{1,0:T(8,128)} %hx_in.1) | copy-start | bytes 1572868
  2.7 1.0 %copy-start.2 = (f32[32,4096]{1,0:T(8,128)S(1)}, f32[32,4096]{1,0:T(8,128)}, u32[]{:S(2)}) copy-start(f32[32,4096]{1,0:T(8,128)} %hz_in.1) | copy-start | bytes 1572868
  3.8 0.7 %copy-start.3 = (s32[4]{0:T(128)S(1)}, s32[4]{0:T(128)}, u32[]{:S(2)}) copy-start(s32[4]{0:T(128)} %shifts_ref.1) | copy-start | bytes 52
  4.4 0.7 %copy-start.4 = (s32[33]{0:T(128)S(1)}, s32[33]{0:T(128)}, u32[]{:S(2)}) copy-start(s32[33]{0:T(128)} %seq_ref.1) | copy-start | bytes 400
  5.1 0.7 %copy-start.5 = (f32[4]{0:T(128)S(1)}, f32[4]{0:T(128)}, u32[]{:S(2)}) copy-start(f32[4]{0:T(128)} %eps_ref.1) | copy-start | bytes 52

commit v2 on v1

--- a/solution.py
+++ b/solution.py
@@ -1,4 +1,5 @@
 import functools
+import math
 
 import jax
 import jax.numpy as jnp
@@ -16,16 +17,17 @@
 PAD = 5
 CHUNK = 4
 REACH = ITERS * SMAX
-EARLY = 2
+FIRST_HOP, LAST_HOP = 3, 6
+EARLY = 6
 
 
 def kernel(
     rows,
     own,
     span,
-    shifts_ref,
-    seq_ref,
-    eps_ref,
+    shifts_in,
+    seq_in,
+    eps_in,
     e_in,
     hx_in,
     hz_in,
@@ -53,6 +55,10 @@
     edge_rows,
     bound_out,
     bound_in,
+    shifts_ref,
+    seq_ref,
+    eps_ref,
+    scalar_sem,
     local_sem,
     edge_send,
     edge_recv,
@@ -62,6 +68,15 @@
     bound_recv_sem,
     relay_send,
     relay_recv,
+    stage_e,
+    stage_hx,
+    stage_hz,
+    stage_bound,
+    stage_recv,
+    stage_bound_recv,
+    forward_send,
+    forward_bound_send,
+    ahead_sem,
 ):
     me = lax.axis_index("gx")
     core = lax.axis_index("gz")
@@ -107,13 +122,63 @@
             local_sem.at[4],
         )
     )
-    for load in loads:
-        load.start()
+    scalars = [
+        pltpu.make_async_copy(source, target, scalar_sem.at[k])
+        for k, (source, target) in enumerate(
+            ((shifts_in, shifts_ref), (seq_in, seq_ref), (eps_in, eps_ref))
+        )
+    ]
+    for copy in scalars + loads:
+        copy.start()
+
+    side = math.isqrt(count)
+    place = lax.rem(me, side)
+    sends = me > 0
+    receives = me < count - 1
+    staged = sends & ((place == 0) | ((me == 1) & (core == 0)))
+    direct = sends & ~staged
+    fed = me < count - side
+    hop_first = fed & (place == FIRST_HOP)
+    hop_last = (fed & (place == LAST_HOP)) | ((me == 0) & (core == 1))
+    hops = hop_first | hop_last
+    stage_target = {
+        "gx": jnp.where(me == 1, 0, me - side + FIRST_HOP),
+        "gz": jnp.where(me == 1, 1, core),
+    }
+    next_target = {"gx": me + (LAST_HOP - FIRST_HOP)}
+    last_target = {
+        "gx": jnp.where(me == 0, 0, me + (side - 1 - LAST_HOP)),
+        "gz": jnp.where(me == 0, 0, core),
+    }
+    flow_core = jnp.where(me == 0, 0, core)
 
     barrier = pltpu.get_barrier_semaphore()
-    pl.semaphore_signal(barrier, inc=1, device_id=to_right, device_id_type=MESH)
+
+    def greet(condition, target):
+        @pl.when(condition)
+        def _():
+            pl.semaphore_signal(barrier, inc=1, device_id=target, device_id_type=MESH)
+
+    greet(receives & (place < side - 1) & (me > 0), to_right)
+    greet((me == 0) & (core == 1), {"gx": 1, "gz": 0})
+    greet((me == 0) & (core == 1), {"gx": 1, "gz": 1})
+    greet(hop_first, {"gx": me + side - FIRST_HOP})
     pl.semaphore_signal(barrier, inc=1, device_id=to_partner, device_id_type=MESH)
-    pl.semaphore_wait(barrier, 2)
+
+    @pl.when(sends)
+    def _():
+        pl.semaphore_wait(barrier, 2)
+
+    @pl.when(~sends)
+    def _():
+        pl.semaphore_wait(barrier, 1)
+
+    def tell(condition):
+        @pl.when(condition)
+        def _():
+            pl.semaphore_signal(ahead_sem, inc=1, device_id=to_left, device_id_type=MESH)
+
+    tell(fed & ((place == side - 1) | (place == LAST_HOP)))
 
     edge = (1 - core) * (own - 1)
     halo = jnp.where(core == 1, PAD + own, PAD - 1)
@@ -125,23 +190,64 @@
             src_ref=src, dst_ref=dst, send_sem=send, recv_sem=recv, device_id=target, device_id_type=MESH
         )
 
-    def bulk(f, first, width, slot):
-        source = pl.ds(pl.multiple_of(first * LANE, LANE), width * LANE)
-        target = pl.ds(pl.multiple_of((first + PAD) * LANE, LANE), width * LANE)
-        return remote(
-            ins[f].at[pl.ds(0, REACH), source],
-            start[f].at[pl.ds(rows, REACH), target],
-            send_sem.at[f, slot],
-            recv_sem.at[f, slot],
-            to_left,
-        )
-
-    def chunk_copy(f, j):
-        if isinstance(j, int) and j == chunks - 1:
-            return bulk(f, core + j * CHUNK, CHUNK - 1, j)
-        return bulk(f, core + j * CHUNK, CHUNK, j)
-
-    edge_copies = [bulk(f, edge, 1, chunks) for f in range(3)]
+    stages = (stage_e, stage_hx, stage_hz)
+
+    def columns(flow, slot, shift):
+        if isinstance(slot, int) and slot == chunks:
+            first, tiles = (1 - flow) * (own - 1), 1
+        else:
+            tiles = CHUNK - 1 if isinstance(slot, int) and slot == chunks - 1 else CHUNK
+            first = flow + slot * CHUNK
+        return pl.ds(pl.multiple_of((first + shift) * LANE, LANE), tiles * LANE)
+
+    def piece(f, slot, kind, handed=False):
+        flow = flow_core if handed else core
+        here_at = columns(flow, slot, 0)
+        source = stages[f].at[:, here_at] if handed else ins[f].at[pl.ds(0, REACH), here_at]
+        if kind == "direct":
+            target = start[f].at[pl.ds(rows, REACH), columns(flow, slot, PAD)]
+            device = last_target if handed else to_left
+            arrived = recv_sem
+        else:
+            target = stages[f].at[:, here_at]
+            device = next_target if handed else stage_target
+            arrived = stage_recv
+        sent = forward_send if handed else send_sem
+        return remote(source, target, sent.at[f, slot], arrived.at[f, slot], device)
+
+    def bound_piece(kind, handed=False):
+        source = stage_bound if handed else bound_out.at[:, mine]
+        sent = forward_bound_send if handed else bound_send_sem
+        if kind == "direct":
+            device = last_target if handed else to_left
+            return remote(source, bound_in.at[:, mine], sent, bound_recv_sem, device)
+        device = next_target if handed else stage_target
+        return remote(source, stage_bound, sent, stage_bound_recv, device)
+
+    def send(slots, bound=False):
+        for condition, kind in ((direct, "direct"), (staged, "stage")):
+
+            @pl.when(condition)
+            def _(kind=kind):
+                if bound:
+                    bound_piece(kind).start()
+                for slot in slots:
+                    for f in range(3):
+                        piece(f, slot, kind).start()
+
+    def hand_on(slots, bound=False):
+        for condition, kind in ((hop_first, "stage"), (hop_last, "direct")):
+
+            @pl.when(condition)
+            def _(kind=kind):
+                for slot in slots:
+                    for f in range(3):
+                        piece(f, slot, "stage", True).wait_recv()
+                        piece(f, slot, kind, True).start()
+                if bound:
+                    bound_piece("stage", True).wait_recv()
+                    bound_piece(kind, True).start()
+
     partner_copies = [
         remote(
             ins[f].at[:, at(edge)],
@@ -170,13 +276,19 @@
             to_partner,
         )
     )
-    for copy in edge_copies:
-        copy.start()
     for copy in partner_copies:
         copy.start()
-    for j in range(EARLY):
-        for f in range(3):
-            chunk_copy(f, j).start()
+    send([chunks] + list(range(EARLY)))
+
+    between = fed & (place > FIRST_HOP) & (place < LAST_HOP)
+
+    @pl.when(between)
+    def _():
+        pl.semaphore_wait(ahead_sem, 1)
+
+    tell(between)
+    for copy in scalars:
+        copy.wait()
 
     lane = lax.broadcasted_iota(jnp.int32, (8, LANE), 1)
     sub = lax.broadcasted_iota(jnp.int32, (8, LANE), 0)
@@ -300,15 +412,18 @@
             advance(j, s, strip, False)
         return carry
 
-    lax.fori_loop(0, chunks + 1, strip_chunk, 0)
+    @pl.when(sends)
+    def _():
+        lax.fori_loop(0, chunks + 1, strip_chunk, 0)
+
     gain_bands([r for r in range(bands) if r not in strip])
-    bound_copy = remote(
-        bound_out.at[:, mine], bound_in.at[:, mine], bound_send_sem, bound_recv_sem, to_left
-    )
-    bound_copy.start()
-    for j in range(EARLY, chunks):
-        for f in range(3):
-            chunk_copy(f, j).start()
+    send(range(EARLY, chunks), bound=True)
+
+    @pl.when(fed & ((place == FIRST_HOP) | (place == LAST_HOP)))
+    def _():
+        pl.semaphore_wait(ahead_sem, 1)
+
+    hand_on([chunks] + list(range(EARLY)), bound=True)
 
     relays = [
         remote(
@@ -329,13 +444,16 @@
             to_partner,
         )
     )
-    for f in range(3):
-        edge_copies[f].wait_recv()
-        relays[f].start()
-    bound_copy.wait_recv()
-    relays[3].start()
-    for copy in relays:
-        copy.wait_recv()
+
+    @pl.when(receives)
+    def _():
+        for f in range(3):
+            piece(f, chunks, "direct").wait_recv()
+            relays[f].start()
+        bound_piece("direct").wait_recv()
+        relays[3].start()
+        for copy in relays:
+            copy.wait_recv()
 
     moved = offsets[-1]
     turn = jnp.bitwise_and(moved, 7)
@@ -363,22 +481,26 @@
         for s in range(1, ITERS + 1):
             advance(j, s, everything, True)
 
-    def first_chunk():
-        for f in range(3):
-            chunk_copy(f, 0).wait_recv()
-        main_chunk(jnp.int32(0))
+    def arrive(j):
+        @pl.when(receives)
+        def _():
+            for f in range(3):
+                piece(f, j, "direct").wait_recv()
 
     def middle(j, carry):
-        for f in range(3):
-            chunk_copy(f, j).wait_recv()
+        arrive(j)
         main_chunk(j)
         finish(j)
         return carry
 
-    first_chunk()
-    lax.fori_loop(1, chunks - 1, middle, 0)
-    for f in range(3):
-        chunk_copy(f, chunks - 1).wait_recv()
+    arrive(0)
+    main_chunk(jnp.int32(0))
+    lax.fori_loop(1, EARLY, middle, 0)
+    for j in range(EARLY, chunks - 1):
+        hand_on([j])
+        middle(jnp.int32(j), 0)
+    hand_on([chunks - 1])
+    arrive(chunks - 1)
 
     def closing(j, carry):
         main_chunk(j)
@@ -387,11 +509,35 @@
 
     lax.fori_loop(chunks - 1, chunks + 1, closing, 0)
 
-    for copy in edge_copies + partner_copies + relays + [bound_copy]:
+    for copy in partner_copies:
         copy.wait_send()
-    for j in range(chunks):
-        for f in range(3):
-            chunk_copy(f, j).wait_send()
+
+    @pl.when(receives)
+    def _():
+        for copy in relays:
+            copy.wait_send()
+
+    for condition, handed in ((sends, False), (hops, True)):
+
+        @pl.when(condition)
+        def _(handed=handed):
+            bound_piece("direct", handed).wait_send()
+            for slot in range(chunks + 1):
+                for f in range(3):
+                    piece(f, slot, "direct", handed).wait_send()
+
+
+def store(e_in, hx_in, hz_in, e_out, hx_out, hz_out, sem):
+    copies = [
+        pltpu.make_async_copy(source, target, sem.at[k])
+        for k, (source, target) in enumerate(
+            ((e_in, e_out), (hx_in, hx_out), (hz_in, hz_out))
+        )
+    ]
+    for copy in copies:
+        copy.start()
+    for copy in copies:
+        copy.wait()
 
 
 def body(electric, magnetic_x, magnetic_z, index_map, period_seq, eps_table, shifts):
@@ -403,14 +549,13 @@
     types, span, _ = index_map.shape
     field = pltpu.VMEM((total, width), jnp.float32)
     dma = pltpu.SemaphoreType.DMA
-    hbm = pl.BlockSpec(memory_space=pl.ANY)
-    smem = pl.BlockSpec(memory_space=pltpu.SMEM)
+    hbm = pl.BlockSpec(memory_space=pltpu.HBM)
     vmem = pl.BlockSpec(memory_space=pltpu.VMEM)
     out = jax.ShapeDtypeStruct((rows, cells), jnp.float32)
-    return pl.pallas_call(
+    fields = pl.pallas_call(
         functools.partial(kernel, rows, own, span),
         out_shape=(out, out, out),
-        in_specs=[smem, smem, smem, hbm, hbm, hbm, hbm],
+        in_specs=[hbm] * 7,
         out_specs=(vmem, vmem, vmem),
         scratch_shapes=[field] * 16
         + [
@@ -418,6 +563,10 @@
             pltpu.VMEM((types, total, LANE), jnp.int32),
             pltpu.VMEM((ITERS, width), jnp.float32),
             pltpu.VMEM((ITERS, width), jnp.float32),
+            pltpu.SMEM(shifts.shape, jnp.int32),
+            pltpu.SMEM(period_seq.shape, jnp.int32),
+            pltpu.SMEM(eps_table.shape, jnp.float32),
+            dma((3,)),
             dma((5,)),
             dma((5,)),
             dma((5,)),
@@ -427,12 +576,35 @@
             dma,
             dma((4,)),
             dma((4,)),
+        ]
+        + [pltpu.VMEM((REACH, cells), jnp.float32)] * 3
+        + [
+            pltpu.VMEM((ITERS, cells), jnp.float32),
+            dma((3, chunks + 1)),
+            dma,
+            dma((3, chunks + 1)),
+            dma,
+            pltpu.SemaphoreType.REGULAR,
         ],
         compiler_params=pltpu.CompilerParams(
             collective_id=0, has_side_effects=True, vmem_limit_bytes=48 * 1024 * 1024
         ),
         name="yee",
-    )(shifts, period_seq, eps_table, electric, magnetic_x, magnetic_z, index_map)
+    )(
+        *(
+            pltpu.with_memory_space_constraint(x, pltpu.HBM)
+            for x in (shifts, period_seq, eps_table, electric, magnetic_x, magnetic_z, index_map)
+        )
+    )
+    return pl.pallas_call(
+        store,
+        out_shape=(out, out, out),
+        in_specs=[pl.BlockSpec(memory_space=pl.ANY)] * 3,
+        out_specs=[hbm] * 3,
+        scratch_shapes=[dma((3,))],
+        compiler_params=pltpu.CompilerParams(vmem_limit_bytes=1024 * 1024),
+        name="store",
+    )(*fields)
 
 
 def solution(mesh):

time: 53.3 us -> 37.9 us (0.71)
  the two profiles are of different devices: /device:TPU:513 before, /device:TPU:631 now
where the time goes in v2:
time: 37.9 us; the launch traced here: 37.8 us
  Pallas kernels  37.1 us (98%)
  between operations  0.64 us (2%)
    pallas_call x1, Pallas kernels, body(): pl.pallas_call(functools.partial(kernel, rows, own, span), out_shape=(out...  36 us
    pallas_call x1, Pallas kernels, body(): pl.pallas_call(store, out_shape=(out, out, out), in_specs=[pl.BlockSpec(m...  1.17 us

profile of v2, /device:TPU:631, one launch (start us, length us, event | category | flops | bytes accessed | tf_op | source)
XLA Modules:
  0.0 37.8 jit_solution(8232307230902898908)
XLA Ops:
  0.6 36.0 %yee.1 = (f32[32,4096]{1,0:T(8,128)S(1)}, f32[32,4096]{1,0:T(8,128)S(1)}, f32[32,4096]{1,0:T(8,128)S(1)}) custom-call(s32[4]{0:T(128)} %shifts_in.1, s32[33]{0:T(128)} %seq_in.1, f32[4]{0:T(128)} %eps_in.1, f32[32,4096]{1,0:T(8,128)} %e_in.1, f32[32,4096]{1,0:T(8,128)} %hx_in.1, f32[32,4096]{1,0:T(8,128)} %hz_in.1, s32[4,64,4096]{2,1,0:T(8,128)} %map_in.1), custom_call_target="tpu_custom_call" | custom-call | tf_op jit(solution)/shard_map/yee/pallas_call | solution.py:555
  36.6 1.2 %store.1 = (f32[32,4096]{1,0:T(8,128)}, f32[32,4096]{1,0:T(8,128)}, f32[32,4096]{1,0:T(8,128)}) custom-call(f32[32,4096]{1,0:T(8,128)S(1)} %get-tuple-element.6.e_in, f32[32,4096]{1,0:T(8,128)S(1)} %get-tuple-element.7.hx_in, f32[32,4096]{1,0:T(8,128)S(1)} %get-tuple-element.8.hz_in), custom_call_target="tpu_custom_call" | custom-call | tf_op jit(solution)/shard_map/store/pallas_call | solution.py:599

commit v3 on v2

--- a/solution.py
+++ b/solution.py
@@ -18,6 +18,7 @@
 CHUNK = 4
 REACH = ITERS * SMAX
 FIRST_HOP, LAST_HOP = 3, 6
+HANDED = 4
 EARLY = 6
 
 
@@ -135,19 +136,19 @@
     place = lax.rem(me, side)
     sends = me > 0
     receives = me < count - 1
-    staged = sends & ((place == 0) | ((me == 1) & (core == 0)))
-    direct = sends & ~staged
-    fed = me < count - side
-    hop_first = fed & (place == FIRST_HOP)
-    hop_last = (fed & (place == LAST_HOP)) | ((me == 0) & (core == 1))
-    hops = hop_first | hop_last
+    through = (me == 1) & (core == 0)
+    direct = sends & ~through
+    crossing = sends & (place == 0)
+    hop_start = (me == 0) & (core == 1)
+    hop_first = (me >= side) & (place == FIRST_HOP)
+    hop_last = (me >= side) & (place == LAST_HOP)
     stage_target = {
-        "gx": jnp.where(me == 1, 0, me - side + FIRST_HOP),
+        "gx": jnp.where(me == 1, 0, me + FIRST_HOP),
         "gz": jnp.where(me == 1, 1, core),
     }
     next_target = {"gx": me + (LAST_HOP - FIRST_HOP)}
     last_target = {
-        "gx": jnp.where(me == 0, 0, me + (side - 1 - LAST_HOP)),
+        "gx": jnp.where(me == 0, 0, me - LAST_HOP - 1),
         "gz": jnp.where(me == 0, 0, core),
     }
     flow_core = jnp.where(me == 0, 0, core)
@@ -159,26 +160,30 @@
         def _():
             pl.semaphore_signal(barrier, inc=1, device_id=target, device_id_type=MESH)
 
-    greet(receives & (place < side - 1) & (me > 0), to_right)
-    greet((me == 0) & (core == 1), {"gx": 1, "gz": 0})
-    greet((me == 0) & (core == 1), {"gx": 1, "gz": 1})
-    greet(hop_first, {"gx": me + side - FIRST_HOP})
+    greet(receives & (me > 0), to_right)
+    greet(hop_start, {"gx": 1, "gz": 0})
+    greet(hop_start, {"gx": 1, "gz": 1})
+    greet(hop_first, {"gx": me - FIRST_HOP})
+    row_end = (me >= side) & (place == side - 1)
+    greet(receives & (place == side - 1), {"gx": me + side})
     pl.semaphore_signal(barrier, inc=1, device_id=to_partner, device_id_type=MESH)
 
-    @pl.when(sends)
-    def _():
-        pl.semaphore_wait(barrier, 2)
-
-    @pl.when(~sends)
-    def _():
-        pl.semaphore_wait(barrier, 1)
+    for condition, amount in (
+        (~sends, 1),
+        (sends & ~(crossing | row_end), 2),
+        (crossing | row_end, 3),
+    ):
+
+        @pl.when(condition)
+        def _(amount=amount):
+            pl.semaphore_wait(barrier, amount)
 
     def tell(condition):
         @pl.when(condition)
         def _():
             pl.semaphore_signal(ahead_sem, inc=1, device_id=to_left, device_id_type=MESH)
 
-    tell(fed & ((place == side - 1) | (place == LAST_HOP)))
+    tell(hop_last | row_end)
 
     edge = (1 - core) * (own - 1)
     halo = jnp.where(core == 1, PAD + own, PAD - 1)
@@ -225,28 +230,35 @@
         return remote(source, stage_bound, sent, stage_bound_recv, device)
 
     def send(slots, bound=False):
-        for condition, kind in ((direct, "direct"), (staged, "stage")):
-
-            @pl.when(condition)
-            def _(kind=kind):
-                if bound:
+        if bound:
+            for condition, kind in ((direct, "direct"), (through, "stage")):
+
+                @pl.when(condition)
+                def _(kind=kind):
                     bound_piece(kind).start()
-                for slot in slots:
+
+        for slot in slots:
+            whole = slot == chunks or slot < HANDED
+            for condition, kind in (
+                (direct if whole else direct & ~crossing, "direct"),
+                (through if whole else through | crossing, "stage"),
+            ):
+
+                @pl.when(condition)
+                def _(kind=kind, slot=slot):
                     for f in range(3):
                         piece(f, slot, kind).start()
 
-    def hand_on(slots, bound=False):
-        for condition, kind in ((hop_first, "stage"), (hop_last, "direct")):
-
-            @pl.when(condition)
-            def _(kind=kind):
-                for slot in slots:
-                    for f in range(3):
-                        piece(f, slot, "stage", True).wait_recv()
-                        piece(f, slot, kind, True).start()
-                if bound:
-                    bound_piece("stage", True).wait_recv()
-                    bound_piece(kind, True).start()
+    def hand_on(condition, kind, slots, bound=False):
+        @pl.when(condition)
+        def _():
+            for slot in slots:
+                for f in range(3):
+                    piece(f, slot, "stage", True).wait_recv()
+                    piece(f, slot, kind, True).start()
+            if bound:
+                bound_piece("stage", True).wait_recv()
+                bound_piece(kind, True).start()
 
     partner_copies = [
         remote(
@@ -280,7 +292,38 @@
         copy.start()
     send([chunks] + list(range(EARLY)))
 
-    between = fed & (place > FIRST_HOP) & (place < LAST_HOP)
+    relays = [
+        remote(
+            start[f].at[pl.ds(rows, REACH), at(edge + PAD)],
+            start[f].at[pl.ds(rows, REACH), at(halo)],
+            relay_send.at[f],
+            relay_recv.at[f],
+            to_partner,
+        )
+        for f in range(3)
+    ]
+    relays.append(
+        remote(
+            bound_in.at[:, at(edge + PAD)],
+            bound_in.at[:, at(halo)],
+            relay_send.at[3],
+            relay_recv.at[3],
+            to_partner,
+        )
+    )
+
+    def pass_edge(condition):
+        @pl.when(condition)
+        def _():
+            for f in range(3):
+                piece(f, chunks, "direct").wait_recv()
+                relays[f].start()
+            bound_piece("direct").wait_recv()
+            relays[3].start()
+
+    pass_edge(hop_start)
+    hand_on(hop_start, "direct", [chunks] + list(range(EARLY)), bound=True)
+    between = (me >= side) & (place > FIRST_HOP) & (place < LAST_HOP)
 
     @pl.when(between)
     def _():
@@ -419,41 +462,48 @@
     gain_bands([r for r in range(bands) if r not in strip])
     send(range(EARLY, chunks), bound=True)
 
-    @pl.when(fed & ((place == FIRST_HOP) | (place == LAST_HOP)))
+    @pl.when(hop_first | hop_last)
     def _():
         pl.semaphore_wait(ahead_sem, 1)
 
-    hand_on([chunks] + list(range(EARLY)), bound=True)
-
-    relays = [
-        remote(
-            start[f].at[pl.ds(rows, REACH), at(edge + PAD)],
-            start[f].at[pl.ds(rows, REACH), at(halo)],
-            relay_send.at[f],
-            relay_recv.at[f],
-            to_partner,
-        )
-        for f in range(3)
-    ]
-    relays.append(
-        remote(
-            bound_in.at[:, at(edge + PAD)],
-            bound_in.at[:, at(halo)],
-            relay_send.at[3],
-            relay_recv.at[3],
-            to_partner,
-        )
-    )
-
-    @pl.when(receives)
+    hand_on(hop_first, "stage", range(HANDED, chunks))
+    hand_on(hop_last, "direct", range(HANDED, chunks))
+
+    at_start = (me == 0) & (core == 0)
+
+    pass_edge(receives & (me > 0))
+
+    @pl.when(at_start)
     def _():
         for f in range(3):
             piece(f, chunks, "direct").wait_recv()
-            relays[f].start()
         bound_piece("direct").wait_recv()
-        relays[3].start()
-        for copy in relays:
-            copy.wait_recv()
+
+    @pl.when(receives)
+    def _():
+        @pl.when(~hop_start)
+        def _():
+            for copy in relays:
+                copy.wait_recv()
+
+        @pl.when(hop_start)
+        def _():
+            theirs = columns(0, chunks, 0)
+            copies = [
+                pltpu.make_async_copy(
+                    stages[f].at[:, theirs], start[f].at[pl.ds(rows, REACH), at(here)], local_sem.at[f]
+                )
+                for f in range(3)
+            ]
+            copies.append(
+                pltpu.make_async_copy(
+                    stage_bound.at[:, theirs], bound_in.at[:, at(here)], local_sem.at[3]
+                )
+            )
+            for copy in copies:
+                copy.start()
+            for copy in copies:
+                copy.wait()
 
     moved = offsets[-1]
     turn = jnp.bitwise_and(moved, 7)
@@ -497,9 +547,9 @@
     main_chunk(jnp.int32(0))
     lax.fori_loop(1, EARLY, middle, 0)
     for j in range(EARLY, chunks - 1):
-        hand_on([j])
+        hand_on(hop_start, "direct", [j])
         middle(jnp.int32(j), 0)
-    hand_on([chunks - 1])
+    hand_on(hop_start, "direct", [chunks - 1])
     arrive(chunks - 1)
 
     def closing(j, carry):
@@ -512,19 +562,23 @@
     for copy in partner_copies:
         copy.wait_send()
 
-    @pl.when(receives)
+    @pl.when(receives & ~at_start)
     def _():
         for copy in relays:
             copy.wait_send()
 
-    for condition, handed in ((sends, False), (hops, True)):
-
+    def drain(condition, handed, slots, bound):
         @pl.when(condition)
-        def _(handed=handed):
-            bound_piece("direct", handed).wait_send()
-            for slot in range(chunks + 1):
+        def _():
+            if bound:
+                bound_piece("direct", handed).wait_send()
+            for slot in slots:
                 for f in range(3):
                     piece(f, slot, "direct", handed).wait_send()
+
+    drain(sends, False, range(chunks + 1), True)
+    drain(hop_start, True, range(chunks + 1), True)
+    drain(hop_first | hop_last, True, range(HANDED, chunks), False)
 
 
 def store(e_in, hx_in, hz_in, e_out, hx_out, hz_out, sem):

time: 37.9 us -> 32.7 us (0.86)
  the two profiles are of different devices: /device:TPU:631 before, /device:TPU:513 now
where the time goes in v3:
time: 32.7 us; the launch traced here: 32.6 us
  Pallas kernels  32 us (98%)
  between operations  0.64 us (2%)
    pallas_call x1, Pallas kernels, body(): pl.pallas_call(functools.partial(kernel, rows, own, span), out_shape=(out...  30.8 us
    pallas_call x1, Pallas kernels, body(): pl.pallas_call(store, out_shape=(out, out, out), in_specs=[pl.BlockSpec(m...  1.17 us

profile of v3, /device:TPU:513, one launch (start us, length us, event | category | flops | bytes accessed | tf_op | source)
XLA Modules:
  0.0 32.6 jit_solution(9267388626039648964)
XLA Ops:
  0.6 30.8 %yee.1 = (f32[32,4096]{1,0:T(8,128)S(1)}, f32[32,4096]{1,0:T(8,128)S(1)}, f32[32,4096]{1,0:T(8,128)S(1)}) custom-call(s32[4]{0:T(128)} %shifts_in.1, s32[33]{0:T(128)} %seq_in.1, f32[4]{0:T(128)} %eps_in.1, f32[32,4096]{1,0:T(8,128)} %e_in.1, f32[32,4096]{1,0:T(8,128)} %hx_in.1, f32[32,4096]{1,0:T(8,128)} %hz_in.1, s32[4,64,4096]{2,1,0:T(8,128)} %map_in.1), custom_call_target="tpu_custom_call" | custom-call | tf_op jit(solution)/shard_map/yee/pallas_call | solution.py:609
  31.4 1.2 %store.1 = (f32[32,4096]{1,0:T(8,128)}, f32[32,4096]{1,0:T(8,128)}, f32[32,4096]{1,0:T(8,128)}) custom-call(f32[32,4096]{1,0:T(8,128)S(1)} %get-tuple-element.6.e_in, f32[32,4096]{1,0:T(8,128)S(1)} %get-tuple-element.7.hx_in, f32[32,4096]{1,0:T(8,128)S(1)} %get-tuple-element.8.hz_in), custom_call_target="tpu_custom_call" | custom-call | tf_op jit(solution)/shard_map/store/pallas_call | solution.py:653

commit v4 on v3

--- a/solution.py
+++ b/solution.py
@@ -18,8 +18,8 @@
 CHUNK = 4
 REACH = ITERS * SMAX
 FIRST_HOP, LAST_HOP = 3, 6
-HANDED = 4
-EARLY = 6
+HANDED = 6
+EARLY = 3
 
 
 def kernel(
@@ -168,6 +168,42 @@
     greet(receives & (place == side - 1), {"gx": me + side})
     pl.semaphore_signal(barrier, inc=1, device_id=to_partner, device_id_type=MESH)
 
+    def gain_bands(which, own_tiles, edge_tile):
+        gains = [COURANT * (1.0 / jnp.full((8, LANE), eps_ref[k], jnp.float32)) for k in range(4)]
+        periods = (me * rows // span, (me * rows + rows) // span)
+        designs = [jnp.full((8, LANE), seq_ref[p], jnp.int32) for p in periods]
+
+        def gain_tile(source, r, tile, target):
+            design = designs[0] if r < own_bands else designs[1]
+            maps = [source[k, pl.ds(8 * r, 8), at(tile)] for k in range(source.shape[0])]
+            level = maps[0]
+            for k in range(1, len(maps)):
+                level = jnp.where(design == k, maps[k], level)
+            coeff[pl.ds(8 * r, 8), at(target)] = jnp.where(
+                level < 2,
+                jnp.where(level == 0, gains[0], gains[1]),
+                jnp.where(level == 2, gains[2], gains[3]),
+            )
+
+        def one_tile(tile, carry):
+            for r in which:
+                gain_tile(design_rows, r, tile, tile + PAD)
+            return carry
+
+        if own_tiles:
+            lax.fori_loop(0, own, one_tile, 0, unroll=2)
+        if edge_tile:
+            for r in which:
+                gain_tile(edge_rows, r, 0, here)
+
+    here = jnp.where(core == 0, PAD + own, PAD - 1)
+
+    @pl.when(hop_start)
+    def _():
+        for copy in scalars + loads:
+            copy.wait()
+        gain_bands(range(bands), True, False)
+
     for condition, amount in (
         (~sends, 1),
         (sends & ~(crossing | row_end), 2),
@@ -187,7 +223,6 @@
 
     edge = (1 - core) * (own - 1)
     halo = jnp.where(core == 1, PAD + own, PAD - 1)
-    here = jnp.where(core == 0, PAD + own, PAD - 1)
     outside = jnp.where(core == 1, PAD + own, PAD - 1)
 
     def remote(src, dst, send, recv, target):
@@ -241,7 +276,7 @@
             whole = slot == chunks or slot < HANDED
             for condition, kind in (
                 (direct if whole else direct & ~crossing, "direct"),
-                (through if whole else through | crossing, "stage"),
+                (through, "stage"),
             ):
 
                 @pl.when(condition)
@@ -290,6 +325,12 @@
     )
     for copy in partner_copies:
         copy.start()
+    @pl.when(crossing)
+    def _():
+        for slot in range(HANDED, chunks):
+            for f in range(3):
+                piece(f, slot, "stage").start()
+
     send([chunks] + list(range(EARLY)))
 
     relays = [
@@ -330,8 +371,11 @@
         pl.semaphore_wait(ahead_sem, 1)
 
     tell(between)
-    for copy in scalars:
-        copy.wait()
+
+    @pl.when(~hop_start)
+    def _():
+        for copy in scalars:
+            copy.wait()
 
     lane = lax.broadcasted_iota(jnp.int32, (8, LANE), 1)
     sub = lax.broadcasted_iota(jnp.int32, (8, LANE), 0)
@@ -346,36 +390,6 @@
     for f in range(3):
         for r in range(bands):
             start[f][pl.ds(8 * r, 8), at(outside)] = zero
-
-    gains = [COURANT * (1.0 / jnp.full((8, LANE), eps_ref[k], jnp.float32)) for k in range(4)]
-    period = me * rows // span
-    next_period = (me * rows + rows) // span
-    designs = [jnp.full((8, LANE), seq_ref[p], jnp.int32) for p in (period, next_period)]
-
-    def gain_of(level):
-        return jnp.where(
-            level < 2,
-            jnp.where(level == 0, gains[0], gains[1]),
-            jnp.where(level == 2, gains[2], gains[3]),
-        )
-
-    def gain_tile(source, r, tile, target):
-        design = designs[0] if r < own_bands else designs[1]
-        maps = [source[k, pl.ds(8 * r, 8), at(tile)] for k in range(source.shape[0])]
-        level = maps[0]
-        for k in range(1, len(maps)):
-            level = jnp.where(design == k, maps[k], level)
-        coeff[pl.ds(8 * r, 8), at(target)] = gain_of(level)
-
-    def gain_bands(which):
-        def body(tile, carry):
-            for r in which:
-                gain_tile(design_rows, r, tile, tile + PAD)
-            return carry
-
-        lax.fori_loop(0, own, body, 0, unroll=2)
-        for r in which:
-            gain_tile(edge_rows, r, 0, here)
 
     def load(ref, r, tile):
         return ref[pl.ds(8 * r, 8), at(tile)]
@@ -444,11 +458,14 @@
             hx_low = hx_new
 
     strip = [REACH // 8 - 1, REACH // 8]
-    for load_copy in loads:
-        load_copy.wait()
+    @pl.when(~hop_start)
+    def _():
+        for copy in loads:
+            copy.wait()
+
     for copy in partner_copies:
         copy.wait_recv()
-    gain_bands(strip)
+    gain_bands(range(bands), False, True)
 
     def strip_chunk(j, carry):
         for s in range(1, ITERS):
@@ -457,19 +474,22 @@
 
     @pl.when(sends)
     def _():
+        gain_bands(strip, True, False)
         lax.fori_loop(0, chunks + 1, strip_chunk, 0)
-
-    gain_bands([r for r in range(bands) if r not in strip])
+        gain_bands([r for r in range(bands) if r not in strip], True, False)
+
+    at_start = (me == 0) & (core == 0)
+
+    @pl.when(at_start)
+    def _():
+        gain_bands(range(bands), True, False)
+
     send(range(EARLY, chunks), bound=True)
 
     @pl.when(hop_first | hop_last)
     def _():
         pl.semaphore_wait(ahead_sem, 1)
 
-    hand_on(hop_first, "stage", range(HANDED, chunks))
-    hand_on(hop_last, "direct", range(HANDED, chunks))
-
-    at_start = (me == 0) & (core == 0)
 
     pass_edge(receives & (me > 0))
 
@@ -538,17 +558,17 @@
                 piece(f, j, "direct").wait_recv()
 
     def middle(j, carry):
+        hand_on(hop_last & (j == EARLY), "direct", range(HANDED, chunks))
+        hand_on(hop_start & (j >= EARLY), "direct", [j])
         arrive(j)
         main_chunk(j)
         finish(j)
         return carry
 
+    hand_on(hop_first, "stage", range(HANDED, chunks))
     arrive(0)
     main_chunk(jnp.int32(0))
-    lax.fori_loop(1, EARLY, middle, 0)
-    for j in range(EARLY, chunks - 1):
-        hand_on(hop_start, "direct", [j])
-        middle(jnp.int32(j), 0)
+    lax.fori_loop(1, chunks - 1, middle, 0)
     hand_on(hop_start, "direct", [chunks - 1])
     arrive(chunks - 1)
 

time: 32.7 us -> 32.5 us (level)
  no operation moved by 1% of the time
where the time goes in v4:
time: 32.5 us; the launch traced here: 32.4 us
  Pallas kernels  31.8 us (98%)
  between operations  0.64 us (2%)
    pallas_call x1, Pallas kernels, body(): pl.pallas_call(functools.partial(kernel, rows, own, span), out_shape=(out...  30.6 us
    pallas_call x1, Pallas kernels, body(): pl.pallas_call(store, out_shape=(out, out, out), in_specs=[pl.BlockSpec(m...  1.17 us

profile of v4, /device:TPU:513, one launch (start us, length us, event | category | flops | bytes accessed | tf_op | source)
XLA Modules:
  0.0 32.4 jit_solution(16901088746555220887)
XLA Ops:
  0.6 30.6 %yee.1 = (f32[32,4096]{1,0:T(8,128)S(1)}, f32[32,4096]{1,0:T(8,128)S(1)}, f32[32,4096]{1,0:T(8,128)S(1)}) custom-call(s32[4]{0:T(128)} %shifts_in.1, s32[33]{0:T(128)} %seq_in.1, f32[4]{0:T(128)} %eps_in.1, f32[32,4096]{1,0:T(8,128)} %e_in.1, f32[32,4096]{1,0:T(8,128)} %hx_in.1, f32[32,4096]{1,0:T(8,128)} %hz_in.1, s32[4,64,4096]{2,1,0:T(8,128)} %map_in.1), custom_call_target="tpu_custom_call" | custom-call | tf_op jit(solution)/shard_map/yee/pallas_call | solution.py:629
  31.2 1.2 %store.1 = (f32[32,4096]{1,0:T(8,128)}, f32[32,4096]{1,0:T(8,128)}, f32[32,4096]{1,0:T(8,128)}) custom-call(f32[32,4096]{1,0:T(8,128)S(1)} %get-tuple-element.6.e_in, f32[32,4096]{1,0:T(8,128)S(1)} %get-tuple-element.7.hx_in, f32[32,4096]{1,0:T(8,128)S(1)} %get-tuple-element.8.hz_in), custom_call_target="tpu_custom_call" | custom-call | tf_op jit(solution)/shard_map/store/pallas_call | solution.py:673

commit v5 on v4

--- a/solution.py
+++ b/solution.py
@@ -129,8 +129,14 @@
             ((shifts_in, shifts_ref), (seq_in, seq_ref), (eps_in, eps_ref))
         )
     ]
-    for copy in scalars + loads:
+    at_start = (me == 0) & (core == 0)
+    for copy in scalars:
         copy.start()
+
+    @pl.when(~at_start)
+    def _():
+        for copy in loads:
+            copy.start()
 
     side = math.isqrt(count)
     place = lax.rem(me, side)
@@ -325,6 +331,11 @@
     )
     for copy in partner_copies:
         copy.start()
+
+    @pl.when(at_start)
+    def _():
+        for copy in loads:
+            copy.start()
     @pl.when(crossing)
     def _():
         for slot in range(HANDED, chunks):
@@ -478,8 +489,6 @@
         lax.fori_loop(0, chunks + 1, strip_chunk, 0)
         gain_bands([r for r in range(bands) if r not in strip], True, False)
 
-    at_start = (me == 0) & (core == 0)
-
     @pl.when(at_start)
     def _():
         gain_bands(range(bands), True, False)

time: 32.5 us -> 32.5 us (level)
  no operation moved by 1% of the time
where the time goes in v5:
time: 32.5 us; the launch traced here: 32.4 us
  Pallas kernels  31.8 us (98%)
  between operations  0.64 us (2%)
    pallas_call x1, Pallas kernels, body(): pl.pallas_call(functools.partial(kernel, rows, own, span), out_shape=(out...  30.6 us
    pallas_call x1, Pallas kernels, body(): pl.pallas_call(store, out_shape=(out, out, out), in_specs=[pl.BlockSpec(m...  1.17 us

profile of v5, /device:TPU:513, one launch (start us, length us, event | category | flops | bytes accessed | tf_op | source)
XLA Modules:
  0.0 32.4 jit_solution(3051997321289790699)
XLA Ops:
  0.6 30.6 %yee.1 = (f32[32,4096]{1,0:T(8,128)S(1)}, f32[32,4096]{1,0:T(8,128)S(1)}, f32[32,4096]{1,0:T(8,128)S(1)}) custom-call(s32[4]{0:T(128)} %shifts_in.1, s32[33]{0:T(128)} %seq_in.1, f32[4]{0:T(128)} %eps_in.1, f32[32,4096]{1,0:T(8,128)} %e_in.1, f32[32,4096]{1,0:T(8,128)} %hx_in.1, f32[32,4096]{1,0:T(8,128)} %hz_in.1, s32[4,64,4096]{2,1,0:T(8,128)} %map_in.1), custom_call_target="tpu_custom_call" | custom-call | tf_op jit(solution)/shard_map/yee/pallas_call | solution.py:638
  31.3 1.2 %store.1 = (f32[32,4096]{1,0:T(8,128)}, f32[32,4096]{1,0:T(8,128)}, f32[32,4096]{1,0:T(8,128)}) custom-call(f32[32,4096]{1,0:T(8,128)S(1)} %get-tuple-element.6.e_in, f32[32,4096]{1,0:T(8,128)S(1)} %get-tuple-element.7.hx_in, f32[32,4096]{1,0:T(8,128)S(1)} %get-tuple-element.8.hz_in), custom_call_target="tpu_custom_call" | custom-call | tf_op jit(solution)/shard_map/store/pallas_call | solution.py:682
